TPU v7x, 32 devices: a whole 2x2x4 slice. The times are simulated.
32 devices in a mesh: ea: 8 (over z, y), ba: 4 (over x, core).
Axes of the slice: x: 2, y: 2, z: 4, core: 2. Of those that a mesh axis runs over, the one named last changes fastest.
Arguments:
- entities: float32 [4096, 200], P('ea'), may hold values from -1.5 to 1.5
- entity_history: float32 [4096], P('ea'), may hold values from 0.001 to 0.1
- relations: float32 [256, 200], replicated, may hold values from -6 to 6
- relation_history: float32 [256], replicated, may hold values from 0.001 to 0.1
- edge_ends: int32 [8192, 2], P(('ba', 'ea')), may hold values from 0 to 4095, as said below
- edge_relations: int32 [8192], P(('ba', 'ea')), may hold values from 0 to 255
- negatives: int32 [8192], P(('ba', 'ea')), may hold values from 0 to 4095, as said below
Outputs:
- entity_step: float32 [4096, 200], P('ea')
- entity_squares: float32 [4096], P('ea')
- relation_step: float32 [256, 200], replicated
- relation_squares: float32 [256], replicated
- mean_loss: float32 [1], replicated
Inputs may be any that keep to these rules, and one draw needn't show every extreme that they name: `edge_ends`: every entry is an entity id. In each aligned block of 256 edges at most 48 heads have the same owner shard (id // 512), and some shard has exactly 48; the same holds for the tails. Every entry is an entity id. In each run of 256 consecutive negatives at most 48 have the same owner shard (id // 512), and some shard has exactly 48. `edge_relations`: every entry is a relation id.
All inputs are finite; a program needn't handle non-finite values.
Results may differ from a plain program's by a relative error of at most 0.0003.
Values sent between devices are 32-bit elements.
A program may use at most 64 MiB of HBM per device.

v0:
```python
import jax
import jax.numpy as jnp
from jax import lax
from jax.sharding import PartitionSpec as P

learn_rate = 0.1
adagrad_eps = 1e-10
highest = lax.Precision.HIGHEST


def halves(vectors):
    half_width = vectors.shape[-1] // 2
    return (vectors[..., :half_width], vectors[..., half_width:])


def complex_times(former, latter):
    former_real, former_imag = halves(former)
    latter_real, latter_imag = halves(latter)
    return jnp.concatenate(
        [
            former_real * latter_real - former_imag * latter_imag,
            former_real * latter_imag + former_imag * latter_real,
        ],
        axis=-1,
    )


def conjugate(vectors):
    real_part, imag_part = halves(vectors)
    return jnp.concatenate([real_part, -imag_part], axis=-1)


def adagrad_step(slope_vector, history):
    squares = history + jnp.mean(slope_vector * slope_vector, axis=1)
    return (-learn_rate * slope_vector / (jnp.sqrt(squares)[:, None] + adagrad_eps), squares)


def bucket_slots(node_labels, shard_rows, peer_count, room_limit):
    owners = node_labels // shard_rows
    local_rows = node_labels - owners * shard_rows
    onehot = (owners[:, None] == jnp.arange(peer_count, dtype=jnp.int32)[None, :]).astype(jnp.int32)
    earlier = jnp.cumsum(onehot, axis=0) - onehot
    slot_positions = owners * room_limit + jnp.sum(earlier * onehot, axis=1)
    request = jnp.full((peer_count * room_limit,), -1, jnp.int32).at[slot_positions].set(local_rows)
    return (slot_positions, request.reshape(peer_count, room_limit))


def serve_rows(table, demanded_lookups):
    picked = jnp.take(table, jnp.maximum(demanded_lookups, 0), axis=0)
    return jnp.where((demanded_lookups >= 0)[..., None], picked, 0.0)


def outgoing_rows(slope_vector, slot_positions, peer_count, room_limit):
    buffer_rows = (
        jnp.zeros((peer_count * room_limit, slope_vector.shape[1]), jnp.float32)
        .at[slot_positions]
        .set(slope_vector)
    )
    return buffer_rows.reshape(peer_count, room_limit, slope_vector.shape[1])


def absorb(dense_grad, demanded_lookups, incoming):
    flat_rows = jnp.maximum(demanded_lookups, 0).reshape(-1)
    return dense_grad.at[flat_rows].add(incoming.reshape(-1, incoming.shape[-1]))


def matmul(former, latter):
    return jnp.dot(former, latter, precision=highest, preferred_element_type=jnp.float32)


def spread_back(weights, probe_rows):
    return lax.dot_general(
        weights,
        probe_rows,
        (((0,), (0,)), ((), ())),
        precision=highest,
        preferred_element_type=jnp.float32,
    )


def side_terms(probe_rows, positive, candidates):
    scores = lax.dot_general(
        probe_rows,
        candidates,
        (((1,), (1,)), ((), ())),
        precision=highest,
        preferred_element_type=jnp.float32,
    )
    own_edge = lax.broadcasted_iota(jnp.int32, scores.shape, 1) == lax.broadcasted_iota(
        jnp.int32, scores.shape, 0
    )
    scores = jnp.where(own_edge, -jnp.inf, scores)
    peak = jnp.maximum(jnp.max(scores, axis=1), positive)
    lifted = jnp.exp(scores - peak[:, None])
    struck = jnp.exp(positive - peak)
    normal = struck + jnp.sum(lifted, axis=1)
    loss_sum = jnp.sum(jnp.log(normal) + peak - positive)
    return (loss_sum, lifted / normal[:, None], struck / normal)


def on_device(
    entities, entity_history, relations, relation_history, edge_ends, edge_relations, negatives
):
    peer_count = lax.axis_size("ea")
    shard_rows = entities.shape[0]
    row_width = entities.shape[1]
    edge_count = edge_ends.shape[0]
    negative_count = negatives.shape[0]
    edge_share = edge_count // peer_count
    link_room = edge_share + max(1, edge_share // 2)
    negative_share = negative_count // peer_count
    contrast_room = negative_share + max(1, negative_share // 2)
    desired_items = (edge_ends[:, 0], edge_ends[:, 1], negatives)
    room_limits = (link_room, link_room, contrast_room)
    joint_capacity = sum(room_limits)
    joint_places, joint_request = bucket_slots(
        jnp.concatenate(desired_items), shard_rows, peer_count, joint_capacity
    )
    joint_asked = lax.all_to_all(joint_request, "ea", split_axis=0, concat_axis=0, tiled=True)
    joint_answer = lax.all_to_all(
        serve_rows(entities, joint_asked), "ea", split_axis=0, concat_axis=0, tiled=True
    )
    fetched = joint_answer.reshape(-1, row_width)[joint_places]
    head_rows = fetched[:edge_count]
    tail_rows = fetched[edge_count : 2 * edge_count]
    negative_rows = fetched[2 * edge_count :]
    related = jnp.take(relations, edge_relations, axis=0)
    tail_query = complex_times(head_rows, related)
    head_probe = complex_times(conjugate(related), tail_rows)
    positive = jnp.sum(tail_query * tail_rows, axis=1)
    tail_cands = jnp.concatenate([tail_rows, negative_rows], axis=0)
    head_cands = jnp.concatenate([head_rows, negative_rows], axis=0)
    tail_loss, tail_weight, tail_struck = side_terms(tail_query, positive, tail_cands)
    head_loss, head_weight, head_struck = side_terms(head_probe, positive, head_cands)
    gain = tail_struck + head_struck - 2.0
    tail_back = matmul(tail_weight, tail_cands) + gain[:, None] * tail_rows
    head_back = matmul(head_weight, head_cands)
    tail_spread = spread_back(tail_weight, tail_query)
    head_spread = spread_back(head_weight, head_probe)
    head_grad = complex_times(tail_back, conjugate(related)) + head_spread[:edge_count]
    tail_grad = (
        gain[:, None] * tail_query + complex_times(head_back, related) + tail_spread[:edge_count]
    )
    negative_grad = tail_spread[edge_count:] + head_spread[edge_count:]
    relation_rows = complex_times(tail_back, conjugate(head_rows)) + complex_times(
        conjugate(head_back), tail_rows
    )
    relation_local = jax.ops.segment_sum(
        relation_rows, edge_relations, num_segments=relations.shape[0]
    )
    loss_local = tail_loss + head_loss
    dense_grad = jnp.zeros((shard_rows, row_width), jnp.float32)
    joint_grad = jnp.concatenate([head_grad, tail_grad, negative_grad], axis=0)
    incoming = lax.all_to_all(
        outgoing_rows(joint_grad, joint_places, peer_count, joint_capacity),
        "ea",
        split_axis=0,
        concat_axis=0,
        tiled=True,
    )
    dense_grad = absorb(dense_grad, joint_asked, incoming)
    relation_sum, loss_sum = lax.psum((relation_local, loss_local), ("ea", "ba"))
    relation_step, relation_squares = adagrad_step(relation_sum, relation_history)
    mean_loss = (loss_sum / (2.0 * edge_count * peer_count * lax.axis_size("ba"))).reshape(1)
    summed = lax.psum(dense_grad, "ba")
    entity_step, entity_squares = adagrad_step(summed, entity_history)
    return (entity_step, entity_squares, relation_step, relation_squares, mean_loss)


def solution(mesh):
    placed = (
        P("ea", None),
        P("ea"),
        P(),
        P(),
        P(("ba", "ea"), None),
        P(("ba", "ea")),
        P(("ba", "ea")),
    )
    return jax.shard_map(
        on_device,
        mesh=mesh,
        in_specs=placed,
        out_specs=(P("ea", None), P("ea"), P(), P(), P()),
        check_vma=False,
    )
```

profile of v0, /device:TPU:0, one launch (start us, length us, event | category | flops | bytes accessed | tf_op | source)
XLA Modules:
  0.0 283.6 jit_solution(15245476762388330828)
XLA Ops:
  8.0 0.8 fusion.40
  9.5 1.7 reduce-window.6
  11.7 0.7 multiply_subtract_fusion.6
  12.4 0.7 fusion.25
  13.2 3.4 %scatter_custom_fusion = s32[1152]{0:T(1024)S(1)} fusion(s32[768]{0:T(1024)S(1)} %fusion.25, s32[768]{0:T(1024)S(1)} %get-tuple-element.59, s32[]{:T(128)} %constant.34.clone.1), kind=kCustom, calls=%fused_computation.89 | custom fusion | bytes 4612 | tf_op jit(solution)/shard_map/scatter | solution.py:44
  17.2 7.3 %all-to-all-start = ((s32[8,1,144]{2,1,0:T(1,128)}), s32[8,1,144]{2,1,0:T(1,128)S(1)}, u32[]{:S(2)}, u32[]{:S(2)}) async-start(s32[8,1,144]{2,1,0:T(1,128)} %all_to_all.12), calls=%async_computation | async-start | bytes 16384 | tf_op jit(solution)/shard_map/all_to_all | solution.py:119
  24.5 1.2 copy.54
  25.8 5.3 %all-to-all-done = s32[8,1,144]{2,1,0:T(1,128)S(1)} async-done(((s32[8,1,144]{2,1,0:T(1,128)}), s32[8,1,144]{2,1,0:T(1,128)S(1)}, u32[]{:S(2)}, u32[]{:S(2)}) %all-to-all-start) | async-done | bytes 4640 | tf_op jit(solution)/shard_map/all_to_all | solution.py:119
  31.2 3.3 %gather_fusion = f32[1152,200]{1,0:T(8,128)S(1)} fusion(f32[512,200]{1,0:T(8,128)S(1)} %copy.54, s32[2048]{0:T(1024)S(1)} %pad_clamp_fusion), kind=kCustom, calls=%fused_computation | custom fusion | bytes 1847808 | tf_op jit(solution)/shard_map/jit(_take)/gather | solution.py:49
  34.5 1.3 select_select_fusion
  35.8 3.9 %all-to-all-start.1 = ((f32[8,144,200]{2,1,0:T(8,128)}), f32[8,144,200]{2,1,0:T(8,128)S(1)}, u32[]{:S(2)}, u32[]{:S(2)}) async-start(f32[8,144,200]{2,1,0:T(8,128)} %select_select_fusion), calls=%async_computation.1 | async-start | bytes 2359296 | tf_op jit(solution)/shard_map/all_to_all | solution.py:120
  39.9 1.0 gather_fusion.2
  41.0 25.8 %all-to-all-done.1 = f32[8,144,200]{2,1,0:T(8,128)S(1)} async-done(((f32[8,144,200]{2,1,0:T(8,128)}), f32[8,144,200]{2,1,0:T(8,128)S(1)}, u32[]{:S(2)}, u32[]{:S(2)}) %all-to-all-start.1) | async-done | bytes 921632 | tf_op jit(solution)/shard_map/all_to_all | solution.py:120
  66.9 2.1 gather_fusion.1
  69.8 1.2 fusion.43
  71.0 1.2 fusion.42
  73.1 1.1 fusion.8
  74.3 0.7 fusion.11
  75.0 0.7 fusion.14
  75.7 1.1 convolution_add_fusion
  77.4 6.6 %scatter_custom_fusion.1 = f32[1152,200]{1,0:T(8,128)} fusion(s32[768]{0:T(1024)S(1)} %fusion.25, f32[768,200]{1,0:T(8,128)S(1)} %copy.62, f32[]{:T(128)} %constant.33.clone.1), kind=kCustom, calls=%fused_computation.12 | custom fusion | bytes 921604 | tf_op jit(solution)/shard_map/scatter | solution.py:57
  84.0 3.6 %all-to-all-start.2 = ((f32[8,144,200]{2,1,0:T(8,128)}), f32[8,144,200]{2,1,0:T(8,128)S(1)}, u32[]{:S(2)}, u32[]{:S(2)}) async-start(f32[8,144,200]{2,1,0:T(8,128)} %bitcast.10), calls=%async_computation.2 | async-start | bytes 2359296 | tf_op jit(solution)/shard_map/all_to_all | solution.py:154
  88.0 2.6 scatter_custom_fusion.3
  92.0 45.4 %psum.23 = f32[]{:T(128)} all-reduce(f32[]{:T(128)S(6)} %add.183), channel_id=1, replica_groups=mesh['ea'=8,'ba'=4] {'ea','ba'}, use_global_device_ids=true, to_apply=%region_18.19 | all-reduce | flops 1 | bytes 8 | tf_op jit(solution)/shard_map/psum | solution.py:162
  138.1 89.3 %all-reduce.5.cloned.1.call-done = f32[256,200]{1,0:T(8,128)} async-done(((f32[256,200]{1,0:T(8,128)}), f32[256,200]{1,0:T(8,128)}) %all-reduce.5.cloned.1.call-update) | async-done | bytes 204816 | tf_op jit(solution)/shard_map/psum | solution.py:162
  227.3 1.1 multiply_reduce_fusion.1
  229.0 9.3 %scatter_custom_fusion.2 = f32[512,200]{1,0:T(8,128)} fusion(s32[1152]{0:T(1024)S(1)} %reshape.425, f32[1152,200]{1,0:T(8,128)S(1)} %bitcast.44, f32[]{:T(128)} %constant.33.clone.1), kind=kCustom, calls=%fused_computation.29 | custom fusion | flops 230400 | bytes 409604 | tf_op jit(solution)/shard_map/scatter-add | solution.py:64
  238.5 0.8 copy.65
  239.3 31.8 %all-reduce.3.cloned.1.call-done = f32[512,200]{1,0:T(8,128)} async-done(((f32[512,200]{1,0:T(8,128)}), f32[512,200]{1,0:T(8,128)}) %all-reduce.3.cloned.1.call-update) | async-done | bytes 409616 | tf_op jit(solution)/shard_map/psum | solution.py:165
  271.1 1.2 multiply_reduce_fusion
  272.9 1.2 multiply_divide_fusion
  274.1 0.9 copy.64
  (57 shorter events, 6.5 us)
Async XLA Ops:
  17.2 13.8 %all-to-all-start = ((s32[8,1,144]{2,1,0:T(1,128)}), s32[8,1,144]{2,1,0:T(1,128)S(1)}, u32[]{:S(2)}, u32[]{:S(2)}) async-start(s32[8,1,144]{2,1,0:T(1,128)} %all_to_all.12), calls=%async_computation | async-start | bytes 16384 | tf_op jit(solution)/shard_map/all_to_all | solution.py:119
  35.8 3.9 %copy-start.1 = (f32[256,200]{0,1:T(8,128)S(1)}, f32[256,200]{0,1:T(8,128)}, u32[]{:S(2)}) copy-start(f32[256,200]{0,1:T(8,128)} %param.9) | copy-start | bytes 614404
  35.8 4.0 %copy-start.3 = (s32[256]{0:T(256)S(1)}, s32[256]{0:T(256)}, u32[]{:S(2)}) copy-start(s32[256]{0:T(256)} %param.12) | copy-start | bytes 3076
  35.8 31.1 %all-to-all-start.1 = ((f32[8,144,200]{2,1,0:T(8,128)}), f32[8,144,200]{2,1,0:T(8,128)S(1)}, u32[]{:S(2)}, u32[]{:S(2)}) async-start(f32[8,144,200]{2,1,0:T(8,128)} %select_select_fusion), calls=%async_computation.1 | async-start | bytes 2359296 | tf_op jit(solution)/shard_map/all_to_all | solution.py:120
  84.0 145.0 %all-to-all-start.2 = ((f32[8,144,200]{2,1,0:T(8,128)}), f32[8,144,200]{2,1,0:T(8,128)S(1)}, u32[]{:S(2)}, u32[]{:S(2)}) async-start(f32[8,144,200]{2,1,0:T(8,128)} %bitcast.10), calls=%async_computation.2 | async-start | bytes 2359296 | tf_op jit(solution)/shard_map/all_to_all | solution.py:154
  87.6 140.9 %copy-start.4 = (f32[256]{0:T(256)S(1)}, f32[256]{0:T(256)}, u32[]{:S(2)}) copy-start(f32[256]{0:T(256)} %param.10) | copy-start | bytes 3076
  87.6 139.7 %all-reduce.5.cloned.1.call-start = ((), (), s32[]{:S(2)}) async-start(), calls=%async_computation.4 | async-start | bytes 524288 | tf_op jit(solution)/shard_map/psum | solution.py:162
  90.7 180.5 %all-reduce.3.cloned.1.call-start = ((), (), s32[]{:S(2)}) async-start(), calls=%async_computation.3 | async-start | bytes 1048576 | tf_op jit(solution)/shard_map/psum | solution.py:165
  227.3 11.1 %copy-start = (f32[256,200]{1,0:T(8,128)S(1)}, f32[256,200]{1,0:T(8,128)}, u32[]{:S(2)}) copy-start(f32[256,200]{1,0:T(8,128)} %all-reduce.5.cloned.1.call-done) | copy-start | bytes 614404
  229.0 43.3 %copy-start.2 = (f32[512]{0:T(512)S(1)}, f32[512]{0:T(512)}, u32[]{:S(2)}) copy-start(f32[512]{0:T(512)} %param.8) | copy-start | bytes 6148
Sparse Core Ops, SparseCore 0:
  94.5 132.8 all-reduce.4
Sparse Core Ops, SparseCore 1:
  238.5 32.6 all-reduce.2
where the time goes:
time: 284 us
  waiting for transfers between devices  152 us (54%)
  blocking collectives  45.4 us (16%)
  other arithmetic  23.6 us (8%)
  local copies, waits for them, and re-layouts  22.4 us (8%)
  between operations  18.9 us (7%)
  starting transfers between devices  15.1 us (5%)
  matrix products  5.94 us (2%)
    psum x1, waiting for transfers between devices, on_device(): lax.psum((relation_local, loss_local), ('ea', 'ba'))  89.3 us
    psum x1, blocking collectives, on_device(): lax.psum((relation_local, loss_local), ('ea', 'ba'))  45.4 us
    psum x1, waiting for transfers between devices, on_device(): summed = lax.psum(dense_grad, 'ba')  31.8 us
    all_to_all x1, waiting for transfers between devices, on_device(): lax.all_to_all(serve_rows(entities, joint_asked), 'ea', split_axis=0, con...  25.8 us
    scatter-add x1, other arithmetic, absorb(): dense_grad.at[flat_rows].add(incoming.reshape(-1, incoming.shape[-1]))  9.34 us
    all_to_all x1, starting transfers between devices, on_device(): lax.all_to_all(joint_request, 'ea', split_axis=0, concat_axis=0, tiled=True)  7.31 us
    scatter x1, local copies, waits for them, and re-layouts, outgoing_rows(): buffer_rows = jnp.zeros((peer_count * room_limit, slope_vector.shape[1]),...  6.55 us
  transfers between devices with their start and end apart: 5, of which 4 were waited for; matrix products, arithmetic and copies ran while one was open for 3% of the time, Pallas kernels for 0%

commit v1 on v0

--- a/solution.py
+++ b/solution.py
@@ -162,7 +162,7 @@
     relation_sum, loss_sum = lax.psum((relation_local, loss_local), ("ea", "ba"))
     relation_step, relation_squares = adagrad_step(relation_sum, relation_history)
     mean_loss = (loss_sum / (2.0 * edge_count * peer_count * lax.axis_size("ba"))).reshape(1)
-    summed = lax.psum(dense_grad, "ba")
+    summed = jnp.sum(lax.all_gather(dense_grad, "ba"), axis=0)
     entity_step, entity_squares = adagrad_step(summed, entity_history)
     return (entity_step, entity_squares, relation_step, relation_squares, mean_loss)
 

time: 284 us -> 254 us (0.89)
  waiting for transfers between devices: 152 us -> 128 us
  blocking collectives: 45.4 us -> 38.5 us
    psum x1 -> x0, waiting for transfers between devices: 31.8 us -> none  [on_device(): summed = lax.psum(dense_grad, 'ba')]
    all_to_all x1, waiting for transfers between devices: 0.01 us -> 26.2 us  [on_device(): lax.all_to_all(outgoing_rows(joint_grad, joint_places, peer_count, joint_...]
    psum x1, waiting for transfers between devices: 89.3 us -> 71 us  [on_device(): lax.psum((relation_local, loss_local), ('ea', 'ba'))]
    psum x1, blocking collectives: 45.4 us -> 38.5 us  [on_device(): lax.psum((relation_local, loss_local), ('ea', 'ba'))]
  transfers between devices with their start and end apart: 5 -> 5, of which waited for: 4 -> 4; matrix products, arithmetic and copies ran while one was open for 3% -> 7% of each run, Pallas kernels for 0% -> 0%
where the time goes in v1:
time: 254 us
  waiting for transfers between devices  128 us (50%)
  blocking collectives  38.5 us (15%)
  other arithmetic  24.8 us (10%)
  local copies, waits for them, and re-layouts  22.1 us (9%)
  between operations  18.9 us (7%)
  starting transfers between devices  15.1 us (6%)
  matrix products  5.94 us (2%)
    psum x1, waiting for transfers between devices, on_device(): lax.psum((relation_local, loss_local), ('ea', 'ba'))  71 us
    psum x1, blocking collectives, on_device(): lax.psum((relation_local, loss_local), ('ea', 'ba'))  38.5 us
    all_to_all x1, waiting for transfers between devices, on_device(): lax.all_to_all(outgoing_rows(joint_grad, joint_places, peer_count, joint_...  26.2 us
    all_to_all x1, waiting for transfers between devices, on_device(): lax.all_to_all(serve_rows(entities, joint_asked), 'ea', split_axis=0, con...  25.8 us
    scatter-add x1, other arithmetic, absorb(): dense_grad.at[flat_rows].add(incoming.reshape(-1, incoming.shape[-1]))  9.33 us
    all_to_all x1, starting transfers between devices, on_device(): lax.all_to_all(joint_request, 'ea', split_axis=0, concat_axis=0, tiled=True)  7.31 us
    scatter x1, local copies, waits for them, and re-layouts, outgoing_rows(): buffer_rows = jnp.zeros((peer_count * room_limit, slope_vector.shape[1]),...  6.55 us
    all_to_all x1, waiting for transfers between devices, on_device(): lax.all_to_all(joint_request, 'ea', split_axis=0, concat_axis=0, tiled=True)  5.32 us
  transfers between devices with their start and end apart: 5, of which 4 were waited for; matrix products, arithmetic and copies ran while one was open for 7% of the time, Pallas kernels for 0%

profile of v1, /device:TPU:0, one launch (start us, length us, event | category | flops | bytes accessed | tf_op | source)
XLA Modules:
  0.0 253.7 jit_solution(14805222404088901553)
XLA Ops:
  8.0 0.8 fusion.40
  9.5 1.7 reduce-window.6
  11.7 0.7 multiply_subtract_fusion.6
  12.4 0.7 fusion.25
  13.2 3.4 %scatter_custom_fusion = s32[1152]{0:T(1024)S(1)} fusion(s32[768]{0:T(1024)S(1)} %fusion.25, s32[768]{0:T(1024)S(1)} %get-tuple-element.74, s32[]{:T(128)} %constant.34.clone.1), kind=kCustom, calls=%fused_computation.89 | custom fusion | bytes 4612 | tf_op jit(solution)/shard_map/scatter | solution.py:44
  17.2 7.3 %all-to-all-start = ((s32[8,1,144]{2,1,0:T(1,128)}), s32[8,1,144]{2,1,0:T(1,128)S(1)}, u32[]{:S(2)}, u32[]{:S(2)}) async-start(s32[8,1,144]{2,1,0:T(1,128)} %all_to_all.12), calls=%async_computation | async-start | bytes 16384 | tf_op jit(solution)/shard_map/all_to_all | solution.py:119
  24.5 1.2 copy.99
  25.8 5.3 %all-to-all-done = s32[8,1,144]{2,1,0:T(1,128)S(1)} async-done(((s32[8,1,144]{2,1,0:T(1,128)}), s32[8,1,144]{2,1,0:T(1,128)S(1)}, u32[]{:S(2)}, u32[]{:S(2)}) %all-to-all-start) | async-done | bytes 4640 | tf_op jit(solution)/shard_map/all_to_all | solution.py:119
  31.2 3.3 %gather_fusion = f32[1152,200]{1,0:T(8,128)S(1)} fusion(f32[512,200]{1,0:T(8,128)S(1)} %copy.99, s32[2048]{0:T(1024)S(1)} %pad_clamp_fusion), kind=kCustom, calls=%fused_computation | custom fusion | bytes 1847808 | tf_op jit(solution)/shard_map/jit(_take)/gather | solution.py:49
  34.5 1.3 select_select_fusion
  35.8 3.9 %all-to-all-start.1 = ((f32[8,144,200]{2,1,0:T(8,128)}), f32[8,144,200]{2,1,0:T(8,128)S(1)}, u32[]{:S(2)}, u32[]{:S(2)}) async-start(f32[8,144,200]{2,1,0:T(8,128)} %select_select_fusion), calls=%async_computation.1 | async-start | bytes 2359296 | tf_op jit(solution)/shard_map/all_to_all | solution.py:120
  39.9 1.0 gather_fusion.2
  41.0 25.8 %all-to-all-done.1 = f32[8,144,200]{2,1,0:T(8,128)S(1)} async-done(((f32[8,144,200]{2,1,0:T(8,128)}), f32[8,144,200]{2,1,0:T(8,128)S(1)}, u32[]{:S(2)}, u32[]{:S(2)}) %all-to-all-start.1) | async-done | bytes 921632 | tf_op jit(solution)/shard_map/all_to_all | solution.py:120
  66.9 2.1 gather_fusion.1
  69.8 1.2 fusion.43
  71.0 1.2 fusion.42
  73.1 1.1 fusion.8
  74.3 0.7 fusion.11
  75.0 0.7 fusion.14
  75.7 1.1 convolution_add_fusion
  77.4 6.6 %scatter_custom_fusion.1 = f32[1152,200]{1,0:T(8,128)} fusion(s32[768]{0:T(1024)S(1)} %fusion.25, f32[768,200]{1,0:T(8,128)S(1)} %copy.107, f32[]{:T(128)} %constant.33.clone.1), kind=kCustom, calls=%fused_computation.12 | custom fusion | bytes 921604 | tf_op jit(solution)/shard_map/scatter | solution.py:57
  84.0 3.6 %all-to-all-start.2 = ((f32[8,144,200]{2,1,0:T(8,128)}), f32[8,144,200]{2,1,0:T(8,128)S(1)}, u32[]{:S(2)}, u32[]{:S(2)}) async-start(f32[8,144,200]{2,1,0:T(8,128)} %bitcast.10), calls=%async_computation.2 | async-start | bytes 2359296 | tf_op jit(solution)/shard_map/all_to_all | solution.py:154
  88.0 2.6 %scatter_custom_fusion.3 = f32[256,200]{1,0:T(8,128)} fusion(s32[256]{0:T(256)S(1)} %copy-done.2, f32[256,200]{1,0:T(8,128)S(1)} %copy.110, f32[]{:T(128)} %constant.33.clone.1), kind=kCustom, calls=%fused_computation.40 | custom fusion | flops 51200 | bytes 204804 | tf_op jit(solution)/shard_map/scatter-add | solution.py:148
  90.7 26.2 %all-to-all-done.2 = f32[8,144,200]{2,1,0:T(8,128)S(1)} async-done(((f32[8,144,200]{2,1,0:T(8,128)}), f32[8,144,200]{2,1,0:T(8,128)S(1)}, u32[]{:S(2)}, u32[]{:S(2)}) %all-to-all-start.2) | async-done | bytes 921632 | tf_op jit(solution)/shard_map/all_to_all | solution.py:154
  116.9 9.3 %scatter_custom_fusion.2 = f32[512,200]{1,0:T(8,128)} fusion(s32[1152]{0:T(1024)S(1)} %reshape.425, f32[1152,200]{1,0:T(8,128)S(1)} %bitcast.46, f32[]{:T(128)} %constant.33.clone.1), kind=kCustom, calls=%fused_computation.29 | custom fusion | flops 230400 | bytes 409604 | tf_op jit(solution)/shard_map/scatter-add | solution.py:64
  127.5 38.5 %psum.15 = f32[]{:T(128)} all-reduce(f32[]{:T(128)S(6)} %add.181), channel_id=1, replica_groups=mesh['ea'=8,'ba'=4] {'ea','ba'}, use_global_device_ids=true, to_apply=%region_18.19 | all-reduce | flops 1 | bytes 8 | tf_op jit(solution)/shard_map/psum | solution.py:162
  166.7 71.0 %all-reduce.2.cloned.1.call-done = f32[256,200]{1,0:T(8,128)} async-done(((f32[256,200]{1,0:T(8,128)}), f32[256,200]{1,0:T(8,128)}) %all-reduce.2.cloned.1.call-update) | async-done | bytes 204816 | tf_op jit(solution)/shard_map/psum | solution.py:162
  237.7 1.1 multiply_reduce_fusion.1
  239.3 1.1 multiply_divide_fusion.1
  240.4 0.8 copy.111
  241.2 1.8 reduce_sum.88
  244.3 0.8 multiply_divide_fusion
  (56 shorter events, 7.1 us)
Async XLA Ops:
  17.2 13.8 %all-to-all-start = ((s32[8,1,144]{2,1,0:T(1,128)}), s32[8,1,144]{2,1,0:T(1,128)S(1)}, u32[]{:S(2)}, u32[]{:S(2)}) async-start(s32[8,1,144]{2,1,0:T(1,128)} %all_to_all.12), calls=%async_computation | async-start | bytes 16384 | tf_op jit(solution)/shard_map/all_to_all | solution.py:119
  35.8 3.9 %copy-start = (f32[256,200]{0,1:T(8,128)S(1)}, f32[256,200]{0,1:T(8,128)}, u32[]{:S(2)}) copy-start(f32[256,200]{0,1:T(8,128)} %param.9) | copy-start | bytes 614404
  35.8 4.0 %copy-start.2 = (s32[256]{0:T(256)S(1)}, s32[256]{0:T(256)}, u32[]{:S(2)}) copy-start(s32[256]{0:T(256)} %param.12) | copy-start | bytes 3076
  35.8 31.1 %all-to-all-start.1 = ((f32[8,144,200]{2,1,0:T(8,128)}), f32[8,144,200]{2,1,0:T(8,128)S(1)}, u32[]{:S(2)}, u32[]{:S(2)}) async-start(f32[8,144,200]{2,1,0:T(8,128)} %select_select_fusion), calls=%async_computation.1 | async-start | bytes 2359296 | tf_op jit(solution)/shard_map/all_to_all | solution.py:120
  84.0 32.9 %all-to-all-start.2 = ((f32[8,144,200]{2,1,0:T(8,128)}), f32[8,144,200]{2,1,0:T(8,128)S(1)}, u32[]{:S(2)}, u32[]{:S(2)}) async-start(f32[8,144,200]{2,1,0:T(8,128)} %bitcast.10), calls=%async_computation.2 | async-start | bytes 2359296 | tf_op jit(solution)/shard_map/all_to_all | solution.py:154
  87.6 150.1 %all-reduce.2.cloned.1.call-start = ((), (), s32[]{:S(2)}) async-start(), calls=%async_computation.3 | async-start | bytes 524288 | tf_op jit(solution)/shard_map/psum | solution.py:162
  87.9 150.9 %copy-start.3 = (f32[256]{0:T(256)S(1)}, f32[256]{0:T(256)}, u32[]{:S(2)}) copy-start(f32[256]{0:T(256)} %param.10) | copy-start | bytes 3076
  90.7 150.5 %all-gather.3.cloned.1.call-start = ((), (), s32[]{:S(2)}) async-start(), calls=%async_computation.4 | async-start | bytes 2621440 | tf_op jit(solution)/shard_map/all_gather | solution.py:165
  243.0 0.7 copy-start.1
Sparse Core Ops, SparseCore 0:
  94.4 143.2 all-reduce.1
Sparse Core Ops, SparseCore 1:
  126.3 21.8 all-gather.2
